TPU v7x, 128 devices: a whole 4x4x4 slice. The times are simulated.
128 devices in a mesh: samp: 8 (over x, core), feat: 16 (over z, y).
Axes of the slice: x: 4, y: 4, z: 4, core: 2. Of those that a mesh axis runs over, the one named last changes fastest.
Arguments:
- design: float32 [8192, 65536], P('samp', 'feat'), may hold values from -0.06629126 to 0.06629126
- coefficients: float32 [192, 65536], P(None, 'feat'), may hold values from -4 to 4
- response: float32 [192, 8192], P(None, 'samp'), may hold values from -6 to 6
- active_set: int32 [192, 65536], P(None, 'feat'), may hold values 0 or 1
- lambda_path: float32 [192, 16], P('samp'), may hold values from 0.5 to 4
- lambda_index: int32 [192], P('samp'), may hold values from 1 to 15
Outputs:
- margins: float32 [192, 65536], P('samp', 'feat')
- peak_gradient: float32 [192], P('samp')
- violation: float32 [192], P('samp')
- screen_mass: float32 [192], P('samp')
Inputs may be any that keep to these rules, and one draw needn't show every extreme that they name: `active_set`: 1 marks a feature in the response's active set, 0 one outside it. `lambda_index`: the current point on the response's path; the previous point is the one just below it.
All inputs are finite; a program needn't handle non-finite values. No bound on the sum of `active_set` on one device may be relied on, other than what follows from the above.
Results may differ from a plain program's by a relative error of at most 0.000073.
Values sent between devices are 32-bit elements; how exact they have to be, the bound alone decides.
A program may use at most 128 MiB of HBM per device.

v0:
```python
import jax
import jax.numpy as jnp
from jax import lax
from jax.sharding import PartitionSpec as P

NF = 65536


def from_everyone(array, axis):
    copies = jnp.broadcast_to(array, (lax.axis_size(axis), *array.shape))
    return lax.all_to_all(copies, axis, split_axis=0, concat_axis=0, tiled=True)


def all_in_one(array, axis):
    leaves = jax.tree.leaves(array)
    order = sorted(range(len(leaves)), key=lambda k: -leaves[k].size)
    width = (1, *leaves[order[0]].shape)[-1]
    lines = [
        jnp.pad(leaves[k].reshape(-1), (0, -leaves[k].size % width)).reshape(-1, width)
        for k in order
    ]
    both, at, found = (from_everyone(jnp.concatenate(lines), axis), 0, {})
    for k, line in zip(order, lines):
        piece = both[:, at : at + len(line)].reshape(len(both), -1)
        found[k] = piece[:, : leaves[k].size].reshape(-1, *leaves[k].shape)
        at += len(line)
    numbers = iter(range(len(leaves)))
    return jax.tree.map(lambda _: found[next(numbers)], array)


def combined_pairwise(pieces, combine):
    while len(jax.tree.leaves(pieces)[0]) > 1:
        pieces = jax.vmap(combine)(
            *(jax.tree.map(lambda part: part[side::2], pieces) for side in (0, 1))
        )
    return jax.tree.map(lambda part: part[0], pieces)


def joined_all(array, axis, combine):
    pieces = all_in_one(array, axis)
    return combined_pairwise(pieces, combine)


def combine_stats(earlier, later):
    return (jnp.maximum(earlier[0], later[0]), earlier[1] + later[1], earlier[2] + later[2])


def body(design, coefficients, response, active_set, lambda_path, lambda_index):
    masked = coefficients * active_set.astype(jnp.float32)
    partial_value = lax.dot_general(
        masked,
        design,
        (((1,), (1,)), ((), ())),
        precision=lax.Precision.HIGHEST,
        preferred_element_type=jnp.float32,
    )
    fitted = lax.psum(partial_value, "feat")
    residual = response - fitted
    share_rows = lambda_path.shape[0]
    own_first = lax.axis_index("samp") * share_rows
    gradient = lax.psum_scatter(
        jnp.dot(
            residual, design, precision=lax.Precision.HIGHEST, preferred_element_type=jnp.float32
        ),
        "samp",
        scatter_dimension=0,
        tiled=True,
    )
    own_active = lax.dynamic_slice_in_dim(active_set, own_first, share_rows, 0)
    positions = jnp.arange(lambda_path.shape[1], dtype=jnp.int32)
    picker_now = (positions[None, :] == lambda_index[:, None]).astype(jnp.float32)
    picker_before = (positions[None, :] == lambda_index[:, None] - 1).astype(jnp.float32)
    lambda_new = jnp.sum(lambda_path * picker_now, axis=1)
    lambda_old = jnp.sum(lambda_path * picker_before, axis=1)
    threshold = 2.0 * lambda_new - lambda_old
    magnitude = jnp.abs(gradient)
    margins = magnitude - threshold[:, None]
    local_peak = jnp.max(magnitude, axis=1)
    inactive = 1.0 - own_active.astype(jnp.float32)
    local_violation = (
        jnp.sum(inactive * jnp.maximum(magnitude - lambda_new[:, None], 0.0), axis=1) / NF
    )
    local_mass = jnp.sum(jnp.maximum(margins, 0.0), axis=1) / NF
    peak_gradient, violation, screen_mass = joined_all(
        (local_peak, local_violation, local_mass), "feat", combine_stats
    )
    return (margins, peak_gradient, violation, screen_mass)


def solution(mesh):
    return jax.shard_map(
        body,
        mesh=mesh,
        in_specs=(
            P("samp", "feat"),
            P(None, "feat"),
            P(None, "samp"),
            P(None, "feat"),
            P("samp", None),
            P("samp"),
        ),
        out_specs=(P("samp", "feat"), P("samp"), P("samp"), P("samp")),
        check_vma=False,
    )
```

profile of v0, /device:TPU:0, one launch (start us, length us, event | category | flops | bytes accessed | tf_op | source)
XLA Modules:
  0.0 195.9 jit_solution(5664434413590699596)
XLA Ops:
  7.2 0.0 copy-start
  7.2 0.0 all-reduce.2.cloned.1.call-start
  7.2 22.4 %fusion = f32[192,1024]{1,0:T(8,128)} fusion(f32[1024,4096]{1,0:T(8,128)} %param.6, f32[192,4096]{1,0:T(8,128)} %param.7, s32[192,4096]{1,0:T(8,128)} %param.9), kind=kOutput, calls=%fused_computation | convolution fusion | flops 9665249280 | bytes 23855104 | tf_op jit(solution)/shard_map/dot_general | solution.py:50
  29.6 0.0 all-reduce.2.cloned.1.call-update
  29.6 0.2 reduce-scatter.2.cloned.1.call-start
  29.9 88.9 %all-reduce.2.cloned.1.call-done = f32[192,1024]{1,0:T(8,128)} async-done(((f32[192,1024]{1,0:T(8,128)}), f32[192,1024]{1,0:T(8,128)}) %all-reduce.2.cloned.1.call-update) | async-done | bytes 786448 | tf_op jit(solution)/shard_map/psum | solution.py:57
  118.8 0.0 copy-done
  118.8 16.3 %fusion.3 = f32[192,4096]{1,0:T(8,128)} fusion(f32[1024,4096]{1,0:T(8,128)} %param.6, f32[192,1024]{1,0:T(8,128)S(1)} %copy-done, f32[192,1024]{1,0:T(8,128)} %all-reduce.2.cloned.1.call-done), kind=kOutput, calls=%fused_computation.3 | convolution fusion | flops 9663873024 | bytes 21495808 | tf_op jit(solution)/shard_map/dot_general | solution.py:62
  135.1 0.0 copy-start.2
  135.1 0.0 copy-start.1
  135.1 0.0 reduce-scatter.2.cloned.1.call-update
  135.1 0.6 copy-done.2
  135.8 0.1 copy-done.1
  135.9 34.6 %reduce-scatter.2.cloned.1.call-done = f32[24,4096]{1,0:T(8,128)} async-done(((f32[192,4096]{1,0:T(8,128)}), f32[24,4096]{1,0:T(8,128)}) %reduce-scatter.2.cloned.1.call-update) | async-done | bytes 393232 | tf_op jit(solution)/shard_map/reduce_scatter | solution.py:61
  170.5 2.2 %abs_reduce_fusion = (f32[24]{0:T(128)S(1)}, f32[24]{0:T(128)S(1)}, f32[24]{0:T(128)S(1)}, f32[24,4096]{1,0:T(8,128)}) fusion(f32[24,4096]{1,0:T(8,128)} %reduce-scatter.2.cloned.1.call-done, f32[24]{0:T(128)S(1)} %get-tuple-element.6, s32[192,4096]{1,0:T(8,128)} %param.9, s32[]{:T(128)S(6)} %select_n.3, f32[24]{0:T(128)S(1)} %multiply_subtract_fusion), kind=kLoop, calls=%fused_computation.7 | loop fusion | flops 1081272 | bytes 1180132 | tf_op jit(solution)/shard_map/reduce_max | solution.py:78
  172.7 14.4 %all_to_all.5 = f32[16,3,24]{2,1,0:T(4,128)S(1)} all-to-all(f32[16,3,24]{2,1,0:T(4,128)S(1)} %broadcast_in_dim.2), channel_id=1, replica_groups=mesh['samp'=8,'feat'=16] {'feat'}, dimensions={0} | all-to-all | bytes 9216 | tf_op jit(solution)/shard_map/all_to_all | solution.py:11
  187.5 0.5 maximum_bitcast_fusion
  188.0 0.5 add_bitcast_fusion.1
  188.5 0.5 add_bitcast_fusion
  (34 shorter events, 0.5 us)
Async XLA Ops:
  7.2 111.6 %copy-start = (f32[192,1024]{1,0:T(8,128)S(1)}, f32[192,1024]{1,0:T(8,128)}, u32[]{:S(2)}) copy-start(f32[192,1024]{1,0:T(8,128)} %param.8) | copy-start | bytes 2359300
  7.2 111.6 %all-reduce.2.cloned.1.call-start = ((), (), s32[]{:S(2)}) async-start(), calls=%async_computation.2 | async-start | bytes 1572864 | tf_op jit(solution)/shard_map/psum | solution.py:57
  29.6 140.8 %reduce-scatter.2.cloned.1.call-start = ((), (), s32[]{:S(2)}) async-start(), calls=%async_computation.3 | async-start | bytes 3538944 | tf_op jit(solution)/shard_map/reduce_scatter | solution.py:61
  135.1 0.7 copy-start.2
  135.1 0.7 copy-start.1
Sparse Core Ops, SparseCore 0:
  29.8 88.9 all-reduce.1
  135.3 35.1 reduce-scatter.1
where the time goes:
time: 196 us
  waiting for transfers between devices  124 us (63%)
  matrix products  38.7 us (20%)
  blocking collectives  14.4 us (7%)
  between operations  14.1 us (7%)
  other arithmetic  3.81 us (2%)
    psum x1, waiting for transfers between devices, body(): fitted = lax.psum(partial_value, 'feat')  88.9 us
    reduce_scatter x1, waiting for transfers between devices, body(): lax.psum_scatter(jnp.dot(residual, design, precision=lax.Precision.HIGHES...  34.6 us
    dot_general x1, matrix products, body(): lax.dot_general(masked, design, (((1,), (1,)), ((), ())), precision=lax.P...  22.4 us
    dot_general x1, matrix products, body(): jnp.dot(residual, design, precision=lax.Precision.HIGHEST, preferred_elem...  16.3 us
    all_to_all x1, blocking collectives, from_everyone(): return lax.all_to_all(copies, axis, split_axis=0, concat_axis=0, tiled=True)  14.4 us
  transfers between devices with their start and end apart: 2, of which 2 were waited for; matrix products, arithmetic and copies ran while one was open for 0% of the time, Pallas kernels for 0%

commit v1 on v0

v1 whole, which is shorter than its diff:
```python
import functools

import jax
import jax.numpy as jnp
from jax import lax
from jax.experimental import pallas as pl
from jax.experimental.pallas import tpu as pltpu
from jax.sharding import PartitionSpec as P

NF = 65536
F32 = jnp.float32
BF16 = jnp.bfloat16
CHUNKS = 4
PARTS = 8


def split(value):
    high = value.astype(BF16)
    return high, (value - high.astype(F32)).astype(BF16)


def dot(a, b):
    return jnp.dot(a, b, preferred_element_type=F32)


def kernel(
    design, coefficients, response, active, lpath, lindex,
    margins, stats,
    raw, d_hi, d_lo, coef, act, resp, m_hi, m_lo,
    part, got1, summed, got2, resid, a_hi, a_lo,
    grad, got_core, got_hop, got_end, peers,
    load_sem, s1, r1, s2, r2, s3, r3, sc, rc, sx, rx, st, rt,
):
    samp = lax.axis_index("samp")
    feat = lax.axis_index("feat")
    x, core = samp // 2, samp % 2
    z, y = feat // 4, feat % 4
    rows, samples = response.shape
    features = design.shape[1]
    share = rows // 8
    height = samples // CHUNKS
    slab = rows // 4
    width = features // PARTS
    half = width // 2

    def to(s, f):
        return dict(device_id=(s, f), device_id_type=pl.DeviceIdType.MESH)

    partner = 2 * x + 1 - core
    left = 2 * ((x + 3) % 4) + core
    right = 2 * ((x + 1) % 4) + core

    loads = [
        pltpu.make_async_copy(coefficients, coef, load_sem.at[0]),
        pltpu.make_async_copy(active, act, load_sem.at[1]),
    ]
    for c in range(CHUNKS):
        area = pl.ds(c * height, height)
        loads.append(pltpu.make_async_copy(design.at[area], raw.at[area], load_sem.at[3 + c]))
    loads.append(pltpu.make_async_copy(response, resp, load_sem.at[2]))
    for load in loads:
        load.start()

    barrier = pltpu.get_barrier_semaphore()
    for k in range(1, 16):
        pl.semaphore_signal(barrier, inc=1, **to(samp, (feat + k) % 16))
    for s in (partner, left, right):
        pl.semaphore_signal(barrier, inc=1, **to(s, feat))

    loads[0].wait()
    loads[1].wait()

    def mask_step(b, carry):
        area = pl.ds(pl.multiple_of(b * 512, 512), 512)
        hi, lo = split((coef[:, area] * act[:, area].astype(F32)).T)
        m_hi[area, :] = hi
        m_lo[area, :] = lo
        return carry

    lax.fori_loop(0, features // 512, mask_step, 0)

    def along(color, k):
        return 4 * z + (y + k) % 4 if color == 0 else 4 * ((z + k) % 4) + y

    def place(color):
        return y if color == 0 else z

    def slab_of(a):
        return pl.ds(pl.multiple_of(a * slab, slab), slab)

    def send1(c, color, k):
        a = (place(color) + k) % 4
        return pltpu.make_async_remote_copy(
            part.at[c, color, slab_of(a)], got1.at[c, color, k - 1],
            s1.at[c, color, k - 1], r1.at[c, color, k - 1], **to(samp, along(color, k)))

    def send2(c, color, k):
        return pltpu.make_async_remote_copy(
            summed.at[c, color], got2.at[c, color, k - 1],
            s2.at[c, color, k - 1], r2.at[c, color, k - 1], **to(samp, along(1 - color, k)))

    def lanes_of(c, color):
        return pl.ds(c * height + color * 128, 128)

    def send3(c, color, k):
        area = resid.at[slab_of(place(color)), lanes_of(c, color)]
        return pltpu.make_async_remote_copy(
            area, area,
            s3.at[c, color, k - 1], r3.at[c, color, k - 1], **to(samp, along(color, k)))

    for c in range(CHUNKS):
        loads[2 + c].wait()
        area = pl.ds(c * height, height)
        hi, lo = split(raw[area, :])
        d_hi[area, :] = hi
        d_lo[area, :] = lo
        fitted = dot(d_hi[area, :], m_hi[...]) + dot(d_hi[area, :], m_lo[...]) + dot(d_lo[area, :], m_hi[...])
        fitted = fitted.T
        part[c, 0] = fitted[:, :128]
        part[c, 1] = fitted[:, 128:]
        if c == 0:
            pl.semaphore_wait(barrier, 18)
        for k in (2, 1, 3):
            for color in (0, 1):
                send1(c, color, k).start()

    loads[2 + CHUNKS].wait()
    for c in range(CHUNKS):
        for color in (0, 1):
            for k in (1, 2, 3):
                send1(c, color, k).wait_recv()
            summed[c, color] = (part[c, color, slab_of(place(color)), :] + got1[c, color, 0]) + (
                got1[c, color, 1] + got1[c, color, 2])
            for k in (2, 1, 3):
                send2(c, color, k).start()
    for c in range(CHUNKS):
        for color in (0, 1):
            for k in (1, 2, 3):
                send2(c, color, k).wait_recv()
            total = (summed[c, color] + got2[c, color, 0]) + (got2[c, color, 1] + got2[c, color, 2])
            mine, lanes = slab_of(place(color)), lanes_of(c, color)
            resid[mine, lanes] = resp[mine, lanes] - total
            for k in (2, 1, 3):
                send3(c, color, k).start()
    for c in range(CHUNKS):
        for color in (0, 1):
            for k in (1, 2, 3):
                send3(c, color, k).wait_recv()
        area = pl.ds(c * height, height)
        hi, lo = split(resid[:, area])
        a_hi[:, area] = hi
        a_lo[:, area] = lo

    eye = lax.broadcasted_iota(jnp.int32, (share, share), 0) == lax.broadcasted_iota(jnp.int32, (share, share), 1)
    index = jnp.sum(jnp.where(eye, jnp.broadcast_to(lindex[...], (share, share)).astype(F32), 0.0), axis=1, keepdims=True)
    positions = lax.broadcasted_iota(jnp.int32, lpath.shape, 1).astype(F32)
    path = lpath[...]
    lam_new = jnp.sum(jnp.where(positions == index, path, 0.0), axis=1, keepdims=True)
    lam_old = jnp.sum(jnp.where(positions == index - 1.0, path, 0.0), axis=1, keepdims=True)
    threshold = 2.0 * lam_new - lam_old

    def send_core(q):
        return pltpu.make_async_remote_copy(
            grad.at[q, :, 1 - core], got_core.at[q], sc.at[q], rc.at[q], **to(partner, feat))

    near = pl.ds(0, half)
    far = pl.ds(half, half)
    x_left, x_right, x_far = (x + 3) % 4, (x + 1) % 4, (x + 2) % 4

    def send_x(q, kind):
        source, target, where = (
            (grad.at[q, x_far, core, :, near], got_hop.at[q, 0], left),
            (grad.at[q, x_far, core, :, far], got_hop.at[q, 1], right),
            (grad.at[q, x_left, core, :, far], got_end.at[q, 0, :, far], left),
            (grad.at[q, x_right, core, :, near], got_end.at[q, 1, :, near], right),
            (grad.at[q, x_left, core, :, near], got_end.at[q, 0, :, near], left),
            (grad.at[q, x_right, core, :, far], got_end.at[q, 1, :, far], right),
        )[kind]
        return pltpu.make_async_remote_copy(source, target, sx.at[q, kind], rx.at[q, kind], **to(where, feat))

    def multiply(q):
        cols = pl.ds(q * width, width)
        right_hi = d_hi[:, cols]
        value = dot(a_hi[...], right_hi) + dot(a_lo[...], right_hi) + dot(a_hi[...], d_lo[:, cols])
        for j in range(8):
            grad[q, j // 2, j % 2] = value[j * share:(j + 1) * share, :]
        send_core(q).start()

    def first_hop(q):
        send_core(q).wait_recv()
        for j in range(4):
            grad[q, j, core] = grad[q, j, core] + got_core[q, j]
        for kind in (0, 1, 2, 3):
            send_x(q, kind).start()

    def second_hop(q):
        send_x(q, 0).wait_recv()
        send_x(q, 1).wait_recv()
        grad[q, x_left, core, :, near] = grad[q, x_left, core, :, near] + got_hop[q, 0]
        grad[q, x_right, core, :, far] = grad[q, x_right, core, :, far] + got_hop[q, 1]
        send_x(q, 4).start()
        send_x(q, 5).start()

    own_rows = pl.ds(pl.multiple_of(samp * share, share), share)

    def finish(q, carry):
        peak, violation, mass = carry
        for kind in (2, 3, 4, 5):
            send_x(q, kind).wait_recv()
        cols = pl.ds(q * width, width)
        magnitude = jnp.abs(grad[q, x, core] + (got_end[q, 0] + got_end[q, 1]))
        margin = magnitude - threshold
        margins[:, cols] = margin
        excess = (1.0 - act[own_rows, cols].astype(F32)) * jnp.maximum(magnitude - lam_new, 0.0)
        positive = jnp.maximum(margin, 0.0)
        for j in range(0, width, 128):
            peak = jnp.maximum(peak, magnitude[:, j:j + 128])
            violation = violation + excess[:, j:j + 128]
            mass = mass + positive[:, j:j + 128]
        return peak, violation, mass

    carry = tuple(jnp.zeros((share, 128), F32) for _ in range(3))
    for q in range(PARTS):
        multiply(q)
        if q >= 1:
            first_hop(q - 1)
    first_hop(PARTS - 1)
    for q in range(PARTS):
        second_hop(q)
    for q in range(PARTS):
        carry = finish(q, carry)

    peak, violation, mass = carry
    lane = lax.broadcasted_iota(jnp.int32, (share, 128), 1)
    packed = jnp.where(
        lane == 0, jnp.max(peak, axis=1, keepdims=True),
        jnp.where(
            lane == 1, jnp.sum(violation, axis=1, keepdims=True) * (1.0 / NF),
            jnp.where(lane == 2, jnp.sum(mass, axis=1, keepdims=True) * (1.0 / NF), 0.0)))
    packed = jnp.concatenate([packed, jnp.zeros((128 - share, 128), F32)], axis=0).T
    peers[feat] = packed[:8, :]

    def send_stats(k):
        return pltpu.make_async_remote_copy(
            peers.at[feat], peers.at[feat], st.at[k], rt.at[k], **to(samp, (feat + k) % 16))

    for k in range(1, 16):
        send_stats(k).start()
    for k in range(1, 16):
        send_stats(k).wait_recv()
    everything = [peers[k] for k in range(16)]
    largest, total = everything[0], everything[0]
    for k in range(1, 16):
        largest = jnp.maximum(largest, everything[k])
        total = total + everything[k]
    stats[...] = jnp.where(lax.broadcasted_iota(jnp.int32, (8, 128), 0) == 0, largest, total)

    for c in range(CHUNKS):
        for color in (0, 1):
            for k in (1, 2, 3):
                send1(c, color, k).wait_send()
                send2(c, color, k).wait_send()
                send3(c, color, k).wait_send()
    for q in range(PARTS):
        send_core(q).wait_send()
        for kind in range(6):
            send_x(q, kind).wait_send()
    for k in range(1, 16):
        send_stats(k).wait_send()


def body(design, coefficients, response, active_set, lambda_path, lambda_index):
    samples, features = design.shape
    rows = coefficients.shape[0]
    share = lambda_path.shape[0]
    height, slab, width = samples // CHUNKS, rows // 4, features // PARTS
    vmem = pltpu.VMEM
    dma = pltpu.SemaphoreType.DMA
    everywhere = pl.BlockSpec(memory_space=pl.ANY)
    inside = pl.BlockSpec(memory_space=pltpu.VMEM)
    margins, stats = pl.pallas_call(
        kernel,
        out_shape=(
            jax.ShapeDtypeStruct((share, features), F32),
            jax.ShapeDtypeStruct((8, 128), F32),
        ),
        in_specs=[everywhere] * 4 + [inside] * 2,
        out_specs=(inside, inside),
        scratch_shapes=[
            vmem((samples, features), F32),
            vmem((samples, features), BF16),
            vmem((samples, features), BF16),
            vmem((rows, features), F32),
            vmem((rows, features), jnp.int32),
            vmem((rows, samples), F32),
            vmem((features, rows), BF16),
            vmem((features, rows), BF16),
            vmem((CHUNKS, 2, rows, 128), F32),
            vmem((CHUNKS, 2, 3, slab, 128), F32),
            vmem((CHUNKS, 2, slab, 128), F32),
            vmem((CHUNKS, 2, 3, slab, 128), F32),
            vmem((rows, samples), F32),
            vmem((rows, samples), BF16),
            vmem((rows, samples), BF16),
            vmem((PARTS, 4, 2, share, width), F32),
            vmem((PARTS, 4, share, width), F32),
            vmem((PARTS, 2, share, width // 2), F32),
            vmem((PARTS, 2, share, width), F32),
            vmem((16, 8, 128), F32),
            dma((3 + CHUNKS,)),
            *[dma((CHUNKS, 2, 3))] * 6,
            *[dma((PARTS,))] * 2,
            *[dma((PARTS, 6))] * 2,
            *[dma((16,))] * 2,
        ],
        compiler_params=pltpu.CompilerParams(
            collective_id=0, has_side_effects=True, vmem_limit_bytes=67043328
        ),
    )(design, coefficients, response, active_set, lambda_path, lambda_index.reshape(1, share))
    return margins, stats[0, :share], stats[1, :share], stats[2, :share]


def solution(mesh):
    return jax.shard_map(
        body,
        mesh=mesh,
        in_specs=(
            P("samp", "feat"),
            P(None, "feat"),
            P(None, "samp"),
            P(None, "feat"),
            P("samp", None),
            P("samp"),
        ),
        out_specs=(P("samp", "feat"), P("samp"), P("samp"), P("samp")),
        check_vma=False,
    )
```

time: 196 us -> 68.3 us (0.35)
  waiting for transfers between devices: 124 us -> 0 us
  Pallas kernels: 0 us -> 62.9 us
  matrix products: 38.7 us -> 0 us
  blocking collectives: 14.4 us -> 0 us
  between operations: 14.1 us -> 0.64 us
  other arithmetic: 3.81 us -> 0 us
  local copies, waits for them, and re-layouts: 1.08 us -> 4.45 us
    psum x1 -> x0, waiting for transfers between devices: 88.9 us -> none  [body(): fitted = lax.psum(partial_value, 'feat')]
    pallas_call x0 -> x1, Pallas kernels: none -> 62.9 us  [body(): pl.pallas_call(kernel, out_shape=(jax.ShapeDtypeStruct((share, features),...]
    dot_general x2 -> x0, matrix products: 38.7 us -> none  [the longest x1 22.4 us: body(): lax.dot_general(masked, design, (((1,), (1,)), ((), ())), precision=lax.P...]
    reduce_scatter x1 -> x0, waiting for transfers between devices: 34.6 us -> none  [body(): lax.psum_scatter(jnp.dot(residual, design, precision=lax.Precision.HIGHES...]
    all_to_all x1 -> x0, blocking collectives: 14.4 us -> none  [from_everyone(): return lax.all_to_all(copies, axis, split_axis=0, concat_axis=0, tiled=True)]
    unnamed x6 -> x2, local copies, waits for them, and re-layouts: 0.68 us -> 3.13 us
    reduce_max x1 -> x0, other arithmetic: 2.17 us -> none  [body(): local_peak = jnp.max(magnitude, axis=1)]
  transfers between devices with their start and end apart: 2 -> 0, of which waited for: 2 -> 0; matrix products, arithmetic and copies ran while one was open for 0% -> 0% of each run, Pallas kernels for 0% -> 0%
where the time goes in v1:
time: 68.3 us; the launch traced here: 68 us
  Pallas kernels  62.9 us (92%)
  local copies, waits for them, and re-layouts  4.45 us (7%)
    pallas_call x1, Pallas kernels, body(): pl.pallas_call(kernel, out_shape=(jax.ShapeDtypeStruct((share, features),...  62.9 us
    unnamed x2, local copies, waits for them, and re-layouts  3.13 us

profile of v1, /device:TPU:0, one launch (start us, length us, event | category | flops | bytes accessed | tf_op | source)
XLA Modules:
  0.0 68.0 jit_solution(1204623707375589895)
XLA Ops:
  0.6 1.4 %copy.10.lpath = f32[24,16]{1,0:T(8,128)} copy(f32[24,16]{0,1:T(8,128)} %param.10) | data formatting | bytes 3072 | tf_op args[4]
  2.0 62.9 %shard_map.93 = (f32[24,4096]{1,0:T(8,128)}, f32[8,128]{1,0:T(8,128)}) custom-call(f32[1024,4096]{1,0:T(8,128)} %design.1, f32[192,4096]{1,0:T(8,128)} %coefficients.1, f32[192,1024]{1,0:T(8,128)} %response.1, s32[192,4096]{1,0:T(8,128)} %active.1, f32[24,16]{1,0:T(8,128)} %copy.10.lpath, s32[1,24]{1,0:T(1,128)} %bitcast.7), custom_call_target="tpu_custom_call" | custom-call | tf_op jit(solution)/shard_map/pallas_call | solution.py:281
  64.9 1.3 %slice_bitcast_fusion = (f32[24]{0:T(128)}, f32[24]{0:T(128)}, f32[24]{0:T(128)}) fusion(f32[8,128]{1,0:T(8,128)} %get-tuple-element.7), kind=kLoop, calls=%fused_computation | loop fusion | bytes 576 | tf_op jit(solution)/shard_map/squeeze | solution.py:320
  66.2 1.8 %copy.12 = f32[24,4096]{1,0:T(8,128)} copy(f32[24,4096]{1,0:T(8,128)} %get-tuple-element.15) | data formatting | bytes 786432

commit v2 on v1

v2 whole, which is shorter than its diff:
```python
import functools

import jax
import jax.numpy as jnp
from jax import lax
from jax.experimental import pallas as pl
from jax.experimental.pallas import tpu as pltpu
from jax.sharding import PartitionSpec as P

NF = 65536
F32 = jnp.float32
BF16 = jnp.bfloat16
CHUNKS = 8
LAG = 4
BLOCKS = 4
WIDTHS = (512,) * 8
PARTS = len(WIDTHS)
STARTS = tuple(sum(WIDTHS[:k]) for k in range(PARTS))


def split(value):
    high = value.astype(BF16)
    return high, (value - high.astype(F32)).astype(BF16)


def dot(a, b):
    return jnp.dot(a, b, preferred_element_type=F32)


def kernel(
    design, coefficients, response, active, lpath, lindex,
    margins, stats,
    raw, d_all, coef, act, resp, m_hi, m_lo,
    part, got1, summed, got2, resid, a_all,
    grad, got_core, got_hop, got_end, lams, peers,
    coef_sem, act_sem, load_sem, sent, r1, r2, r3, rc, rx, rt,
):
    samp = lax.axis_index("samp")
    feat = lax.axis_index("feat")
    x, core = samp // 2, samp % 2
    z, y = feat // 4, feat % 4
    rows, samples = response.shape
    features = design.shape[1]
    share = rows // 8
    height = samples // CHUNKS
    slab = rows // 8

    def to(s, f):
        return dict(device_id=(s, f), device_id_type=pl.DeviceIdType.MESH)

    partner = 2 * x + 1 - core
    left = 2 * ((x + 3) % 4) + core
    right = 2 * ((x + 1) % 4) + core

    step = features // BLOCKS

    def load_block(b):
        area = pl.ds(pl.multiple_of(b * step, step), step)
        return (
            pltpu.make_async_copy(coefficients.at[:, area], coef.at[:, area], coef_sem.at[b]),
            pltpu.make_async_copy(active.at[:, area], act.at[:, area], act_sem.at[b]))

    def load_design(c):
        area = pl.ds(pl.multiple_of(c * height, height), height)
        return pltpu.make_async_copy(design.at[area], raw.at[area], load_sem.at[c])

    load_response = pltpu.make_async_copy(response, resp, load_sem.at[CHUNKS])
    for b in range(BLOCKS):
        for load in load_block(b):
            load.start()

    barrier = pltpu.get_barrier_semaphore()
    for k in range(1, 16):
        pl.semaphore_signal(barrier, inc=1, **to(samp, (feat + k) % 16))
    for s in (partner, left, right):
        pl.semaphore_signal(barrier, inc=1, **to(s, feat))

    eye = lax.broadcasted_iota(jnp.int32, (share, share), 0) == lax.broadcasted_iota(jnp.int32, (share, share), 1)
    positions = lax.broadcasted_iota(jnp.int32, lpath.shape, 0)
    index, path = lindex[...], lpath[...]

    def pick(chosen):
        row = jnp.sum(jnp.where(positions == chosen, path, 0.0), axis=0, keepdims=True)
        return jnp.sum(jnp.where(eye, jnp.broadcast_to(row, (share, share)), 0.0), axis=1, keepdims=True)

    lam_new, lam_old = pick(index), pick(index - 1)
    lams[0] = jnp.broadcast_to(lam_new, (share, 128))
    lams[1] = jnp.broadcast_to(2.0 * lam_new - lam_old, (share, 128))

    @jax.named_scope("mask")
    def mask_step(b, carry):
        for load in load_block(b):
            load.wait()
        area = pl.ds(pl.multiple_of(b * step, step), step)
        hi, lo = split((coef[:, area] * act[:, area].astype(F32)).T)
        m_hi[area, :] = hi
        m_lo[area, :] = lo
        return carry

    lax.fori_loop(0, 1, mask_step, 0)
    load_design(0).start()
    lax.fori_loop(1, 2, mask_step, 0)
    load_design(1).start()
    lax.fori_loop(2, BLOCKS, mask_step, 0)
    for c in range(2, CHUNKS):
        load_design(c).start()
    load_response.start()

    def along(color, k):
        return 4 * z + (y + k) % 4 if color == 0 else 4 * ((z + k) % 4) + y

    def place(color):
        return y if color == 0 else z

    def slab_of(color, a):
        return pl.ds(pl.multiple_of((color * 4 + a) * slab, slab), slab)

    def lanes_of(c):
        return pl.ds(pl.multiple_of(c * height, height), height)

    def send1(c, color, k):
        a = (place(color) + k) % 4
        return pltpu.make_async_remote_copy(
            part.at[c, slab_of(color, a)], got1.at[c, color, k - 1],
            sent.at[0], r1.at[c], **to(samp, along(color, k)))

    def send2(c, color, k):
        return pltpu.make_async_remote_copy(
            summed.at[c, color], got2.at[c, color, k - 1],
            sent.at[1], r2.at[c], **to(samp, along(1 - color, k)))

    def send3(c, color, k):
        area = resid.at[slab_of(color, place(color)), lanes_of(c)]
        return pltpu.make_async_remote_copy(
            area, area,
            sent.at[2], r3.at[c], **to(samp, along(color, k)))

    def await_bytes(ref, sem):
        pltpu.make_async_copy(ref, ref, sem).wait()

    def phase1(c):
        await_bytes(got1.at[c], r1.at[c])
        for color in (0, 1):
            summed[c, color] = (part[c, slab_of(color, place(color)), :] + got1[c, color, 0]) + (
                got1[c, color, 1] + got1[c, color, 2])
            for k in (2, 1, 3):
                send2(c, color, k).start()

    def phase2(c):
        await_bytes(got2.at[c], r2.at[c])
        for color in (0, 1):
            total = (summed[c, color] + got2[c, color, 0]) + (got2[c, color, 1] + got2[c, color, 2])
            mine, lanes = slab_of(color, place(color)), lanes_of(c)
            resid[mine, lanes] = resp[mine, lanes] - total
            for k in (2, 1, 3):
                send3(c, color, k).start()

    def phase3(c):
        await_bytes(got2.at[c], r3.at[c])
        hi, lo = split(resid[:, lanes_of(c)])
        a_all[:rows, lanes_of(c)] = hi
        a_all[rows:, lanes_of(c)] = lo

    @jax.named_scope("fit")
    def fit_step(c, carry):
        load_design(c).wait()
        area = pl.ds(pl.multiple_of(c * height, height), height)
        hi, lo = split(raw[area, :])
        d_all[c, 0] = hi
        d_all[c, 1] = lo
        both = dot(d_all[c].reshape(2 * height, features), m_hi[...])
        part[c] = (both[:height] + both[height:] + dot(d_all[c, 0], m_lo[...])).T

        @pl.when(c == 0)
        def _():
            pl.semaphore_wait(barrier, 18)

        for k in (2, 1, 3):
            for color in (0, 1):
                send1(c, color, k).start()

        @pl.when(c >= LAG)
        def _():
            phase1(c - LAG)

        return carry

    lax.fori_loop(0, CHUNKS, fit_step, 0)
    with jax.named_scope("phase12"):
        load_response.wait()
        for c in range(CHUNKS):
            if c + CHUNKS - LAG < CHUNKS:
                phase1(c + CHUNKS - LAG)
            phase2(c)
    x_left, x_right, x_far = (x + 3) % 4, (x + 1) % 4, (x + 2) % 4

    def cols_of(q):
        return pl.ds(STARTS[q], WIDTHS[q])

    def halves_of(q):
        half = WIDTHS[q] // 2
        return pl.ds(STARTS[q], half), pl.ds(STARTS[q] + half, half), pl.ds(STARTS[q] // 2, half)

    def send_core(q):
        return pltpu.make_async_remote_copy(
            grad.at[:, 1 - core, :, cols_of(q)], got_core.at[:, :, cols_of(q)], sent.at[3], rc.at[q], **to(partner, feat))

    def send_x(q, kind):
        near, far, packed = halves_of(q)
        source, target, where = (
            (grad.at[x_far, core, :, near], got_hop.at[0, :, packed], left),
            (grad.at[x_far, core, :, far], got_hop.at[1, :, packed], right),
            (grad.at[x_left, core, :, far], got_end.at[0, :, far], left),
            (grad.at[x_right, core, :, near], got_end.at[1, :, near], right),
            (grad.at[x_left, core, :, near], got_end.at[0, :, near], left),
            (grad.at[x_right, core, :, far], got_end.at[1, :, far], right),
        )[kind]
        return pltpu.make_async_remote_copy(source, target, sent.at[4], rx.at[q, min(kind, 2)], **to(where, feat))

    @jax.named_scope("multiply")
    def multiply(q, first, last):
        cols = cols_of(q)
        depth, width = (last - first) * height, WIDTHS[q]
        left_all = a_all[:, first * height:last * height]
        both = dot(left_all, d_all[first:last, 0, :, cols].reshape(depth, width))
        value = both[:rows] + both[rows:] + dot(left_all[:rows], d_all[first:last, 1, :, cols].reshape(depth, width))
        for j in range(8):
            piece = value[j * share:(j + 1) * share, :]
            if first > 0:
                piece = piece + grad[j // 2, j % 2, :, cols]
            grad[j // 2, j % 2, :, cols] = piece
        if last == CHUNKS:
            send_core(q).start()

    @jax.named_scope("hop1")
    def first_hop(q):
        cols = cols_of(q)
        send_core(q).wait_recv()
        for j in (x_far, x_left, x_right, x):
            grad[j, core, :, cols] = grad[j, core, :, cols] + got_core[j, :, cols]
        for kind in (0, 1, 2, 3):
            send_x(q, kind).start()

    @jax.named_scope("hop2")
    def second_hop(q):
        near, far, packed = halves_of(q)
        send_x(q, 0).wait_recv()
        grad[x_left, core, :, near] = grad[x_left, core, :, near] + got_hop[0, :, packed]
        send_x(q, 4).start()
        send_x(q, 1).wait_recv()
        grad[x_right, core, :, far] = grad[x_right, core, :, far] + got_hop[1, :, packed]
        send_x(q, 5).start()

    own_rows = pl.ds(pl.multiple_of(samp * share, share), share)

    @jax.named_scope("finish")
    def finish(q, carry):
        peak, violation, mass = carry
        await_bytes(got_end.at[:, :, cols_of(q)], rx.at[q, 2])
        for j in range(STARTS[q], STARTS[q] + WIDTHS[q], 128):
            cols = pl.ds(j, 128)
            magnitude = jnp.abs(grad[x, core, :, cols] + (got_end[0, :, cols] + got_end[1, :, cols]))
            margin = magnitude - lams[1]
            margins[:, cols] = margin
            peak = jnp.maximum(peak, magnitude)
            violation = violation + (1.0 - act[own_rows, cols].astype(F32)) * jnp.maximum(magnitude - lams[0], 0.0)
            mass = mass + jnp.maximum(margin, 0.0)
        return peak, violation, mass

    carry = tuple(jnp.zeros((share, 128), F32) for _ in range(3))
    with jax.named_scope("phase3"):
        for c in range(CHUNKS):
            phase3(c)
            if c == CHUNKS // 2:
                multiply(0, 0, CHUNKS // 2)
    multiply(0, CHUNKS // 2, CHUNKS)
    for q in range(PARTS):
        if q >= 1:
            multiply(q, 0, CHUNKS)
            first_hop(q - 1)
    first_hop(PARTS - 1)
    for q in range(PARTS):
        second_hop(q)
    for q in range(PARTS):
        carry = finish(q, carry)

    with jax.named_scope("stats"):
        peak, violation, mass = carry
        lane = lax.broadcasted_iota(jnp.int32, (share, 128), 1)
        packed = jnp.where(
            lane == 0, jnp.max(peak, axis=1, keepdims=True),
            jnp.where(
                lane == 1, jnp.sum(violation, axis=1, keepdims=True) * (1.0 / NF),
                jnp.where(lane == 2, jnp.sum(mass, axis=1, keepdims=True) * (1.0 / NF), 0.0)))
        packed = jnp.concatenate([packed, jnp.zeros((128 - share, 128), F32)], axis=0).T
        peers[feat] = packed[:8, :]

        def send_stats(k):
            return pltpu.make_async_remote_copy(
                peers.at[feat], peers.at[feat], sent.at[5], rt.at[0], **to(samp, (feat + k) % 16))

        for k in range(1, 16):
            send_stats(k).start()
        await_bytes(peers.at[pl.ds(0, 15)], rt.at[0])
        everything = [peers[k] for k in range(16)]
        largest, total = everything[0], everything[0]
        for k in range(1, 16):
            largest = jnp.maximum(largest, everything[k])
            total = total + everything[k]
        stats[...] = jnp.where(lax.broadcasted_iota(jnp.int32, (8, 128), 0) == 0, largest, total)

    await_bytes(got1, sent.at[0])
    await_bytes(got1, sent.at[1])
    await_bytes(got1, sent.at[2])
    await_bytes(got_core, sent.at[3])
    await_bytes(got_hop, sent.at[4])
    await_bytes(got_end, sent.at[4])
    await_bytes(peers.at[pl.ds(0, 15)], sent.at[5])


def body(design, coefficients, response, active_set, lambda_path, lambda_index):
    samples, features = design.shape
    rows = coefficients.shape[0]
    share = lambda_path.shape[0]
    height, slab = samples // CHUNKS, rows // 8
    vmem = pltpu.VMEM
    dma = pltpu.SemaphoreType.DMA
    everywhere = pl.BlockSpec(memory_space=pl.ANY)
    inside = pl.BlockSpec(memory_space=pltpu.VMEM)
    margins, stats = pl.pallas_call(
        kernel,
        out_shape=(
            jax.ShapeDtypeStruct((share, features), F32),
            jax.ShapeDtypeStruct((8, 128), F32),
        ),
        in_specs=[everywhere] * 4 + [inside] * 2,
        out_specs=(inside, inside),
        scratch_shapes=[
            vmem((samples, features), F32),
            vmem((CHUNKS, 2, height, features), BF16),
            vmem((rows, features), F32),
            vmem((rows, features), jnp.int32),
            vmem((rows, samples), F32),
            vmem((features, rows), BF16),
            vmem((features, rows), BF16),
            vmem((CHUNKS, rows, height), F32),
            vmem((CHUNKS, 2, 3, slab, height), F32),
            vmem((CHUNKS, 2, slab, height), F32),
            vmem((CHUNKS, 2, 3, slab, height), F32),
            vmem((rows, samples), F32),
            vmem((2 * rows, samples), BF16),
            vmem((4, 2, share, features), F32),
            vmem((4, share, features), F32),
            vmem((2, share, features // 2), F32),
            vmem((2, share, features), F32),
            vmem((2, share, 128), F32),
            vmem((16, 8, 128), F32),
            dma((BLOCKS,)),
            dma((BLOCKS,)),
            dma((CHUNKS + 1,)),
            dma((6,)),
            *[dma((CHUNKS,))] * 3,
            dma((PARTS,)),
            dma((PARTS, 3)),
            dma((1,)),
        ],
        compiler_params=pltpu.CompilerParams(
            collective_id=0, has_side_effects=True, vmem_limit_bytes=67043328
        ),
    )(design, coefficients, response, active_set, lambda_path.T, lambda_index.reshape(1, share))
    return margins, stats[0, :share], stats[1, :share], stats[2, :share]


def solution(mesh):
    return jax.shard_map(
        body,
        mesh=mesh,
        in_specs=(
            P("samp", "feat"),
            P(None, "feat"),
            P(None, "samp"),
            P(None, "feat"),
            P("samp", None),
            P("samp"),
        ),
        out_specs=(P("samp", "feat"), P("samp"), P("samp"), P("samp")),
        check_vma=False,
    )
```

time: 68.3 us -> 57.6 us (0.84)
  Pallas kernels: 62.9 us -> 53.6 us
  local copies, waits for them, and re-layouts: 4.45 us -> 3.08 us
    pallas_call x1, Pallas kernels: 62.9 us -> 53.6 us  [body(): pl.pallas_call(kernel, out_shape=(jax.ShapeDtypeStruct((share, features),...]
    unnamed x2 -> x1, local copies, waits for them, and re-layouts: 3.13 us -> 1.77 us
where the time goes in v2:
time: 57.6 us; the launch traced here: 57.4 us
  Pallas kernels  53.6 us (93%)
  local copies, waits for them, and re-layouts  3.08 us (5%)
  between operations  0.64 us (1%)
    pallas_call x1, Pallas kernels, body(): pl.pallas_call(kernel, out_shape=(jax.ShapeDtypeStruct((share, features),...  53.6 us
    unnamed x1, local copies, waits for them, and re-layouts  1.77 us
    squeeze x1, local copies, waits for them, and re-layouts, body(): return (margins, stats[0, :share], stats[1, :share], stats[2, :share])  1.32 us

profile of v2, /device:TPU:0, one launch (start us, length us, event | category | flops | bytes accessed | tf_op | source)
XLA Modules:
  0.0 57.4 jit_solution(14932976938949860468)
XLA Ops:
  0.6 53.6 %shard_map.93 = (f32[24,4096]{1,0:T(8,128)}, f32[8,128]{1,0:T(8,128)}) custom-call(f32[1024,4096]{1,0:T(8,128)} %design.1, f32[192,4096]{1,0:T(8,128)} %coefficients.1, f32[192,1024]{1,0:T(8,128)} %response.1, s32[192,4096]{1,0:T(8,128)} %active.1, f32[16,24]{1,0:T(8,128)} %bitcast.8, s32[1,24]{1,0:T(1,128)} %bitcast.9), custom_call_target="tpu_custom_call" | custom-call | tf_op jit(solution)/shard_map/pallas_call | solution.py:330
  54.3 1.3 %slice_bitcast_fusion = (f32[24]{0:T(128)}, f32[24]{0:T(128)}, f32[24]{0:T(128)}) fusion(f32[8,128]{1,0:T(8,128)} %get-tuple-element.7), kind=kLoop, calls=%fused_computation | loop fusion | bytes 576 | tf_op jit(solution)/shard_map/squeeze | solution.py:371
  55.6 1.8 %copy.11 = f32[24,4096]{1,0:T(8,128)} copy(f32[24,4096]{1,0:T(8,128)} %get-tuple-element.15) | data formatting | bytes 786432

commit v3 on v2

v3 whole, which is shorter than its diff:
```python
import functools

import jax
import jax.numpy as jnp
from jax import lax
from jax.experimental import pallas as pl
from jax.experimental.pallas import tpu as pltpu
from jax.sharding import PartitionSpec as P

NF = 65536
F32 = jnp.float32
BF16 = jnp.bfloat16
CHUNKS = 4
GROUPS = ((0, 16), (16, 8))
BLOCKS = 4
PARTS = (8, 4)


def split(value):
    high = value.astype(BF16)
    return high, (value - high.astype(F32)).astype(BF16)


def dot(a, b):
    return jnp.dot(a, b, preferred_element_type=F32)


def kernel(
    design, coefficients, response, active, lpath, lindex,
    margins, stats,
    raw, d_all, coef, act, resp, m_a, m_b,
    part, got1, summed, got2, resid, a_a, a_b,
    grad, got_core, got_hop, got_end, lams, peers, early,
    coef_sem, act_sem, load_sem, sent, r1, r2, r3, rc, rx, rt,
):
    samp = lax.axis_index("samp")
    feat = lax.axis_index("feat")
    x, core = samp // 2, samp % 2
    z, y = feat // 4, feat % 4
    rows, samples = response.shape
    features = design.shape[1]
    share = rows // 8
    height = samples // CHUNKS
    masked, residuals = (m_a, m_b), (a_a, a_b)

    def to(s, f):
        return dict(device_id=(s, f), device_id_type=pl.DeviceIdType.MESH)

    def await_bytes(ref, sem):
        pltpu.make_async_copy(ref, ref, sem).wait()

    def rows_of(g):
        return pl.ds(*GROUPS[g])

    partner = 2 * x + 1 - core
    left = 2 * ((x + 3) % 4) + core
    right = 2 * ((x + 1) % 4) + core

    step = features // BLOCKS

    def load_block(b):
        area = pl.ds(pl.multiple_of(b * step, step), step)
        return (
            pltpu.make_async_copy(coefficients.at[:, area], coef.at[:, area], coef_sem.at[b]),
            pltpu.make_async_copy(active.at[:, area], act.at[:, area], act_sem.at[b]))

    def load_design(c):
        area = pl.ds(pl.multiple_of(c * height, height), height)
        return pltpu.make_async_copy(design.at[area], raw.at[area], load_sem.at[c])

    wide = features // 2

    def load_half(h):
        area = pl.ds(0, height), pl.ds(h * wide, wide)
        return pltpu.make_async_copy(design.at[area], raw.at[area], load_sem.at[h * (CHUNKS + 1)])

    load_response = pltpu.make_async_copy(response, resp, load_sem.at[CHUNKS])
    for h in (0, 1):
        for b in (2 * h, 2 * h + 1):
            for load in load_block(b):
                load.start()
        load_half(h).start()

    barrier = pltpu.get_barrier_semaphore()
    for k in range(1, 16):
        pl.semaphore_signal(barrier, inc=1, **to(samp, (feat + k) % 16))
    for s in (partner, left, right):
        pl.semaphore_signal(barrier, inc=1, **to(s, feat))

    eye = lax.broadcasted_iota(jnp.int32, (share, share), 0) == lax.broadcasted_iota(jnp.int32, (share, share), 1)
    positions = lax.broadcasted_iota(jnp.int32, lpath.shape, 0)
    index, path = lindex[...], lpath[...]

    def pick(chosen):
        row = jnp.sum(jnp.where(positions == chosen, path, 0.0), axis=0, keepdims=True)
        return jnp.sum(jnp.where(eye, jnp.broadcast_to(row, (share, share)), 0.0), axis=1, keepdims=True)

    lam_new, lam_old = pick(index), pick(index - 1)
    lams[0] = jnp.broadcast_to(lam_new, (share, 128))
    lams[1] = jnp.broadcast_to(2.0 * lam_new - lam_old, (share, 128))

    @jax.named_scope("mask")
    def mask_step(b, carry):
        for load in load_block(b):
            load.wait()
        area = pl.ds(pl.multiple_of(b * step, step), step)
        value = coef[:, area] * act[:, area].astype(F32)
        high = value.astype(BF16).astype(F32)
        low = value - high
        for (first, count), target in zip(GROUPS, masked):
            pieces = [
                v.reshape(8, share, step)[:, first:first + count].reshape(8 * count, step).astype(BF16)
                for v in (high, low)]
            target[area, :] = jnp.concatenate(pieces, axis=0).T
        return carry


    def along(color, k):
        return 4 * z + (y + k) % 4 if color == 0 else 4 * ((z + k) % 4) + y

    def place(color):
        return y if color == 0 else z

    def lanes_of(c):
        return pl.ds(pl.multiple_of(c * height, height), height)

    def send1(g, c, color, k):
        j = color * 4 + (place(color) + k) % 4
        return pltpu.make_async_remote_copy(
            part.at[c, j, rows_of(g)], got1.at[c, color, k - 1, rows_of(g)],
            sent.at[0], r1.at[g, c], **to(samp, along(color, k)))

    def send2(g, c, color, k):
        return pltpu.make_async_remote_copy(
            summed.at[c, color, rows_of(g)], got2.at[c, color, k - 1, rows_of(g)],
            sent.at[1], r2.at[g, c], **to(samp, along(1 - color, k)))

    def send3(g, c, color, k):
        area = resid.at[color * 4 + place(color), rows_of(g), lanes_of(c)]
        return pltpu.make_async_remote_copy(
            area, area, sent.at[2], r3.at[g, c], **to(samp, along(color, k)))

    def phase0(g, c, fitted=None):
        count = GROUPS[g][1]
        if fitted is None:
            fitted = dot(d_all[c].reshape(2 * height, features), masked[g][...])
        fitted = (fitted[:height] + fitted[height:]).T
        part[c, :, rows_of(g), :] = (fitted[:8 * count] + fitted[8 * count:]).reshape(8, count, height)

    def start1(g, c):
        for k in (2, 1, 3):
            for color in (0, 1):
                send1(g, c, color, k).start()

    def phase1(g, c):
        mine = rows_of(g)
        await_bytes(got1.at[c, :, :, mine], r1.at[g, c])
        for color in (0, 1):
            summed[c, color, mine] = (part[c, color * 4 + place(color), mine] + got1[c, color, 0, mine]) + (
                got1[c, color, 1, mine] + got1[c, color, 2, mine])
            for k in (2, 1, 3):
                send2(g, c, color, k).start()

    def phase2(g, c):
        first, count = GROUPS[g]
        mine = rows_of(g)
        await_bytes(got2.at[c, :, :, mine], r2.at[g, c])
        for color in (0, 1):
            j = color * 4 + place(color)
            total = (summed[c, color, mine] + got2[c, color, 0, mine]) + (got2[c, color, 1, mine] + got2[c, color, 2, mine])
            observed = resp[pl.ds(pl.multiple_of(j * share + first, 8), count), lanes_of(c)]
            resid[j, mine, lanes_of(c)] = observed - total
            for k in (2, 1, 3):
                send3(g, c, color, k).start()

    def phase3(g, c):
        size = 8 * GROUPS[g][1]
        await_bytes(got2.at[c, :, :, rows_of(g)], r3.at[g, c])
        hi, lo = split(resid[:, rows_of(g), lanes_of(c)].reshape(size, height))
        residuals[g][:size, lanes_of(c)] = hi
        residuals[g][size:, lanes_of(c)] = lo

    @jax.named_scope("fita")
    def fit_a(c, carry):
        load_design(c).wait()
        hi, lo = split(raw[pl.ds(pl.multiple_of(c * height, height), height), :])
        d_all[c, 0] = hi
        d_all[c, 1] = lo
        phase0(0, c)
        start1(0, c)
        return carry

    def fit_half(h):
        lax.fori_loop(2 * h, 2 * h + 2, mask_step, 0)
        with jax.named_scope("half"):
            load_half(h).wait()
            load_design(h + 1).start()
            cols = pl.ds(h * wide, wide)
            hi, lo = split(raw[:height, cols])
            d_all[0, 0, :, cols] = hi
            d_all[0, 1, :, cols] = lo
            return dot(d_all[0, :, :, cols].reshape(2 * height, wide), m_a[cols, :])

    @jax.named_scope("fitb")
    def fit_b(c, carry):
        phase1(0, c)
        phase0(1, c)
        start1(1, c)
        return carry

    early[...] = fit_half(0)
    phase0(0, 0, early[...] + fit_half(1))
    for c in range(3, CHUNKS):
        load_design(c).start()
    load_response.start()
    pl.semaphore_wait(barrier, 18)
    start1(0, 0)
    lax.fori_loop(1, CHUNKS, fit_a, 0)
    load_response.wait()
    lax.fori_loop(0, CHUNKS, fit_b, 0)

    x_left, x_right, x_far = (x + 3) % 4, (x + 1) % 4, (x + 2) % 4
    widths = [features // parts for parts in PARTS]

    def cols_of(g, q):
        return pl.ds(pl.multiple_of(q * widths[g], widths[g]), widths[g])

    def halves_of(g, q):
        width, half = widths[g], widths[g] // 2
        return (
            pl.ds(pl.multiple_of(q * width, half), half),
            pl.ds(pl.multiple_of(q * width + half, half), half),
            pl.ds(pl.multiple_of(q * half, half), half))

    def send_core(g, q):
        return pltpu.make_async_remote_copy(
            grad.at[:, 1 - core, rows_of(g), cols_of(g, q)], got_core.at[:, rows_of(g), cols_of(g, q)],
            sent.at[3], rc.at[g * PARTS[0] + q], **to(partner, feat))

    def send_x(g, q, kind):
        near, far, packed = halves_of(g, q)
        mine = rows_of(g)
        source, target, where = (
            (grad.at[x_far, core, mine, near], got_hop.at[0, mine, packed], left),
            (grad.at[x_far, core, mine, far], got_hop.at[1, mine, packed], right),
            (grad.at[x_left, core, mine, far], got_end.at[0, mine, far], left),
            (grad.at[x_right, core, mine, near], got_end.at[1, mine, near], right),
            (grad.at[x_left, core, mine, near], got_end.at[0, mine, near], left),
            (grad.at[x_right, core, mine, far], got_end.at[1, mine, far], right),
        )[kind]
        return pltpu.make_async_remote_copy(source, target, sent.at[4], rx.at[g * PARTS[0] + q, min(kind // 2, 1)], **to(where, feat))

    @jax.named_scope("multiply")
    def multiply(g, q):
        cols, count, width = cols_of(g, q), GROUPS[g][1], widths[g]
        size = 8 * count
        both = dot(residuals[g][...], d_all[:, 0, :, cols].reshape(samples, width))
        value = both[:size] + both[size:] + dot(residuals[g][:size], d_all[:, 1, :, cols].reshape(samples, width))
        for j in range(8):
            grad[j // 2, j % 2, rows_of(g), cols] = value[j * count:(j + 1) * count, :]
        send_core(g, q).start()

    @jax.named_scope("hop1")
    def first_hop(g, q):
        cols, mine = cols_of(g, q), rows_of(g)
        send_core(g, q).wait_recv()
        for j in (x_far, x_left, x_right, x):
            grad[j, core, mine, cols] = grad[j, core, mine, cols] + got_core[j, mine, cols]
        for kind in (0, 1, 2, 3):
            send_x(g, q, kind).start()

    @jax.named_scope("hop2")
    def second_hop(g, q):
        near, far, packed = halves_of(g, q)
        mine = rows_of(g)
        await_bytes(got_hop.at[:, mine, packed], rx.at[g * PARTS[0] + q, 0])
        grad[x_left, core, mine, near] = grad[x_left, core, mine, near] + got_hop[0, mine, packed]
        grad[x_right, core, mine, far] = grad[x_right, core, mine, far] + got_hop[1, mine, packed]
        send_x(g, q, 4).start()
        send_x(g, q, 5).start()

    @jax.named_scope("finish")
    def finish(g, q, carry):
        peak, violation, mass = carry
        first, count = GROUPS[g]
        mine = rows_of(g)
        await_bytes(got_end.at[:, mine, cols_of(g, q)], rx.at[g * PARTS[0] + q, 1])
        own = pl.ds(pl.multiple_of(samp * share + first, 8), count)
        for j in range(0, widths[g], 128):
            cols = pl.ds(pl.multiple_of(q * widths[g] + j, 128), 128)
            magnitude = jnp.abs(grad[x, core, mine, cols] + (got_end[0, mine, cols] + got_end[1, mine, cols]))
            margin = magnitude - lams[1, mine]
            margins[mine, cols] = margin
            peak = jnp.maximum(peak, magnitude)
            violation = violation + (1.0 - act[own, cols].astype(F32)) * jnp.maximum(magnitude - lams[0, mine], 0.0)
            mass = mass + jnp.maximum(margin, 0.0)
        return peak, violation, mass

    def multiply_a(q, carry):
        multiply(0, q)

        @pl.when(q == 1)
        def _():
            first_hop(0, 0)

        @pl.when(q >= 3)
        def _():
            first_hop(0, q - 2)

        @pl.when(q == 2)
        def _():
            phase2(1, CHUNKS - 1)

        return carry

    def multiply_b(q, carry):
        multiply(1, q)

        @pl.when(q >= 1)
        def _():
            first_hop(1, q - 1)

        second_hop(0, q + 3)
        return carry

    with jax.named_scope("phase12"):
        for c in range(CHUNKS):
            phase2(0, c)
            phase1(1, c)
    with jax.named_scope("phase23"):
        for c in range(CHUNKS):
            if c < CHUNKS - 1:
                phase2(1, c)
            phase3(0, c)
    lax.fori_loop(0, PARTS[0], multiply_a, 0)
    first_hop(0, PARTS[0] - 2)
    first_hop(0, PARTS[0] - 1)

    def second_hops(g, first, last):
        lax.fori_loop(first, last, lambda q, carry: (second_hop(g, q), carry)[1], 0)

    second_hops(0, 0, 3)
    with jax.named_scope("phase3"):
        for c in range(CHUNKS):
            phase3(1, c)
    lax.fori_loop(0, PARTS[1], multiply_b, 0)
    first_hop(1, PARTS[1] - 1)
    second_hops(0, 3 + PARTS[1], PARTS[0])
    second_hops(1, 0, PARTS[1])
    carries = [
        lax.fori_loop(0, PARTS[g], functools.partial(finish, g), (jnp.zeros((count, 128), F32),) * 3)
        for g, (_, count) in enumerate(GROUPS)]
    carry = [jnp.concatenate(pair, axis=0) for pair in zip(*carries)]

    with jax.named_scope("stats"):
        peak, violation, mass = carry
        lane = lax.broadcasted_iota(jnp.int32, (share, 128), 1)
        packed = jnp.where(
            lane == 0, jnp.max(peak, axis=1, keepdims=True),
            jnp.where(
                lane == 1, jnp.sum(violation, axis=1, keepdims=True) * (1.0 / NF),
                jnp.where(lane == 2, jnp.sum(mass, axis=1, keepdims=True) * (1.0 / NF), 0.0)))
        packed = jnp.concatenate([packed, jnp.zeros((128 - share, 128), F32)], axis=0).T
        peers[feat] = packed[:8, :]

        def send_stats(k):
            return pltpu.make_async_remote_copy(
                peers.at[feat], peers.at[feat], sent.at[5], rt.at[0], **to(samp, (feat + k) % 16))

        for k in range(1, 16):
            send_stats(k).start()
        await_bytes(peers.at[pl.ds(0, 15)], rt.at[0])
        everything = [peers[k] for k in range(16)]
        largest, total = everything[0], everything[0]
        for k in range(1, 16):
            largest = jnp.maximum(largest, everything[k])
            total = total + everything[k]
        stats[...] = jnp.where(lax.broadcasted_iota(jnp.int32, (8, 128), 0) == 0, largest, total)

    await_bytes(got1, sent.at[0])
    await_bytes(got1, sent.at[1])
    await_bytes(got1, sent.at[2])
    await_bytes(got_core, sent.at[3])
    await_bytes(got_hop, sent.at[4])
    await_bytes(got_end, sent.at[4])
    await_bytes(peers.at[pl.ds(0, 15)], sent.at[5])


def body(design, coefficients, response, active_set, lambda_path, lambda_index):
    samples, features = design.shape
    rows = coefficients.shape[0]
    share = lambda_path.shape[0]
    height = samples // CHUNKS
    vmem = pltpu.VMEM
    dma = pltpu.SemaphoreType.DMA
    everywhere = pl.BlockSpec(memory_space=pl.ANY)
    inside = pl.BlockSpec(memory_space=pltpu.VMEM)
    margins, stats = pl.pallas_call(
        kernel,
        out_shape=(
            vmem((share, features), F32),
            vmem((8, 128), F32),
        ),
        in_specs=[everywhere] * 4 + [inside] * 2,
        out_specs=(inside, inside),
        scratch_shapes=[
            vmem((samples, features), F32),
            vmem((CHUNKS, 2, height, features), BF16),
            vmem((rows, features), F32),
            vmem((rows, features), jnp.int32),
            vmem((rows, samples), F32),
            *[vmem((features, 16 * count), BF16) for _, count in GROUPS],
            vmem((CHUNKS, 8, share, height), F32),
            vmem((CHUNKS, 2, 3, share, height), F32),
            vmem((CHUNKS, 2, share, height), F32),
            vmem((CHUNKS, 2, 3, share, height), F32),
            vmem((8, share, samples), F32),
            *[vmem((16 * count, samples), BF16) for _, count in GROUPS],
            vmem((4, 2, share, features), F32),
            vmem((4, share, features), F32),
            vmem((2, share, features // 2), F32),
            vmem((2, share, features), F32),
            vmem((2, share, 128), F32),
            vmem((16, 8, 128), F32),
            vmem((2 * height, 16 * GROUPS[0][1]), F32),
            dma((BLOCKS,)),
            dma((BLOCKS,)),
            dma((CHUNKS + 2,)),
            dma((6,)),
            *[dma((2, CHUNKS))] * 3,
            dma((sum(PARTS),)),
            dma((sum(PARTS), 2)),
            dma((1,)),
        ],
        compiler_params=pltpu.CompilerParams(
            collective_id=0, has_side_effects=True, vmem_limit_bytes=62 * 1024 * 1024
        ),
    )(design, coefficients, response, active_set, lambda_path.T, lambda_index.reshape(1, share))
    return margins, stats[0, :share], stats[1, :share], stats[2, :share]


def solution(mesh):
    return jax.shard_map(
        body,
        mesh=mesh,
        in_specs=(
            P("samp", "feat"),
            P(None, "feat"),
            P(None, "samp"),
            P(None, "feat"),
            P("samp", None),
            P("samp"),
        ),
        out_specs=(P("samp", "feat"), P("samp"), P("samp"), P("samp")),
        check_vma=False,
    )
```

time: 57.6 us -> 54.6 us (0.948)
  local copies, waits for them, and re-layouts: 3.08 us -> 1.27 us
  Pallas kernels: 53.6 us -> 52.5 us
    pallas_call x1, Pallas kernels: 53.6 us -> 52.5 us  [body(): pl.pallas_call(kernel, out_shape=(vmem((share, features), F32), vmem((8,...]
    unnamed x1, local copies, waits for them, and re-layouts: 1.77 us -> 0.75 us
    squeeze x1, local copies, waits for them, and re-layouts: 1.32 us -> 0.52 us  [body(): return (margins, stats[0, :share], stats[1, :share], stats[2, :share])]
where the time goes in v3:
time: 54.6 us; the launch traced here: 54.4 us
  Pallas kernels  52.5 us (96%)
  local copies, waits for them, and re-layouts  1.27 us (2%)
  between operations  0.64 us (1%)
    pallas_call x1, Pallas kernels, body(): pl.pallas_call(kernel, out_shape=(vmem((share, features), F32), vmem((8,...  52.5 us

profile of v3, /device:TPU:0, one launch (start us, length us, event | category | flops | bytes accessed | tf_op | source)
XLA Modules:
  0.0 54.4 jit_solution(13139957649718000480)
XLA Ops:
  0.6 52.5 %shard_map.93 = (f32[24,4096]{1,0:T(8,128)S(1)}, f32[8,128]{1,0:T(8,128)S(1)}) custom-call(f32[1024,4096]{1,0:T(8,128)} %design.1, f32[192,4096]{1,0:T(8,128)} %coefficients.1, f32[192,1024]{1,0:T(8,128)} %response.1, s32[192,4096]{1,0:T(8,128)} %active.1, f32[16,24]{1,0:T(8,128)} %bitcast.8, s32[1,24]{1,0:T(1,128)} %bitcast.9), custom_call_target="tpu_custom_call" | custom-call | tf_op jit(solution)/shard_map/pallas_call | solution.py:398
  53.2 0.5 slice_bitcast_fusion
  53.7 0.7 %copy.11 = f32[24,4096]{1,0:T(8,128)} copy(f32[24,4096]{1,0:T(8,128)S(1)} %get-tuple-element.11) | data formatting | bytes 786432

commit v4 on v3

--- a/solution.py
+++ b/solution.py
@@ -75,11 +75,13 @@
         return pltpu.make_async_copy(design.at[area], raw.at[area], load_sem.at[h * (CHUNKS + 1)])
 
     load_response = pltpu.make_async_copy(response, resp, load_sem.at[CHUNKS])
-    for h in (0, 1):
-        for b in (2 * h, 2 * h + 1):
+    def load_blocks(first):
+        for b in (first, first + 1):
             for load in load_block(b):
                 load.start()
-        load_half(h).start()
+
+    load_blocks(0)
+    load_half(0).start()
 
     barrier = pltpu.get_barrier_semaphore()
     for k in range(1, 16):
@@ -191,7 +193,6 @@
         return carry
 
     def fit_half(h):
-        lax.fori_loop(2 * h, 2 * h + 2, mask_step, 0)
         with jax.named_scope("half"):
             load_half(h).wait()
             load_design(h + 1).start()
@@ -208,7 +209,12 @@
         start1(1, c)
         return carry
 
+    lax.fori_loop(0, 1, mask_step, 0)
+    load_blocks(2)
+    lax.fori_loop(1, 2, mask_step, 0)
+    load_half(1).start()
     early[...] = fit_half(0)
+    lax.fori_loop(2, BLOCKS, mask_step, 0)
     phase0(0, 0, early[...] + fit_half(1))
     for c in range(3, CHUNKS):
         load_design(c).start()
@@ -251,22 +257,27 @@
         return pltpu.make_async_remote_copy(source, target, sent.at[4], rx.at[g * PARTS[0] + q, min(kind // 2, 1)], **to(where, feat))
 
     @jax.named_scope("multiply")
-    def multiply(g, q):
+    def multiply(g, q, first=0, last=CHUNKS):
         cols, count, width = cols_of(g, q), GROUPS[g][1], widths[g]
-        size = 8 * count
-        both = dot(residuals[g][...], d_all[:, 0, :, cols].reshape(samples, width))
-        value = both[:size] + both[size:] + dot(residuals[g][:size], d_all[:, 1, :, cols].reshape(samples, width))
+        size, depth = 8 * count, (last - first) * height
+        source = residuals[g][:, first * height:last * height]
+        both = dot(source, d_all[first:last, 0, :, cols].reshape(depth, width))
+        value = both[:size] + both[size:] + dot(source[:size], d_all[first:last, 1, :, cols].reshape(depth, width))
         for j in range(8):
-            grad[j // 2, j % 2, rows_of(g), cols] = value[j * count:(j + 1) * count, :]
-        send_core(g, q).start()
+            piece = value[j * count:(j + 1) * count, :]
+            if first > 0:
+                piece = piece + grad[j // 2, j % 2, rows_of(g), cols]
+            grad[j // 2, j % 2, rows_of(g), cols] = piece
+        if last == CHUNKS:
+            send_core(g, q).start()
 
     @jax.named_scope("hop1")
-    def first_hop(g, q):
+    def first_hop(g, q, kinds=(0, 1, 2, 3)):
         cols, mine = cols_of(g, q), rows_of(g)
         send_core(g, q).wait_recv()
         for j in (x_far, x_left, x_right, x):
             grad[j, core, mine, cols] = grad[j, core, mine, cols] + got_core[j, mine, cols]
-        for kind in (0, 1, 2, 3):
+        for kind in kinds:
             send_x(g, q, kind).start()
 
     @jax.named_scope("hop2")
@@ -313,40 +324,47 @@
 
         return carry
 
-    def multiply_b(q, carry):
-        multiply(1, q)
-
-        @pl.when(q >= 1)
-        def _():
-            first_hop(1, q - 1)
-
-        second_hop(0, q + 3)
-        return carry
-
     with jax.named_scope("phase12"):
         for c in range(CHUNKS):
             phase2(0, c)
             phase1(1, c)
     with jax.named_scope("phase23"):
-        for c in range(CHUNKS):
-            if c < CHUNKS - 1:
+        for c in range(CHUNKS - 1):
+            if c < CHUNKS - 2:
                 phase2(1, c)
             phase3(0, c)
-    lax.fori_loop(0, PARTS[0], multiply_a, 0)
-    first_hop(0, PARTS[0] - 2)
-    first_hop(0, PARTS[0] - 1)
-
-    def second_hops(g, first, last):
-        lax.fori_loop(first, last, lambda q, carry: (second_hop(g, q), carry)[1], 0)
-
-    second_hops(0, 0, 3)
+    multiply(0, 0, 0, CHUNKS - 1)
+    with jax.named_scope("last23"):
+        phase2(1, CHUNKS - 2)
+        phase3(0, CHUNKS - 1)
+    multiply(0, 0, CHUNKS - 1, CHUNKS)
+    lax.fori_loop(1, PARTS[0], multiply_a, 0)
+    second_hop(0, 0)
+    second_hop(0, 1)
     with jax.named_scope("phase3"):
         for c in range(CHUNKS):
             phase3(1, c)
-    lax.fori_loop(0, PARTS[1], multiply_b, 0)
-    first_hop(1, PARTS[1] - 1)
-    second_hops(0, 3 + PARTS[1], PARTS[0])
-    second_hops(1, 0, PARTS[1])
+    multiply(1, 0)
+    first_hop(0, 6)
+    second_hop(0, 2)
+    multiply(1, 1)
+    first_hop(0, 7)
+    second_hop(0, 3)
+    multiply(1, 2)
+    first_hop(1, 0, (0, 1))
+    second_hop(0, 4)
+    multiply(1, 3)
+    first_hop(1, 1, (0, 1))
+    second_hop(0, 5)
+    first_hop(1, 2, (0, 1))
+    first_hop(1, 3, (0, 1))
+    for q in range(PARTS[1]):
+        send_x(1, q, 2).start()
+        send_x(1, q, 3).start()
+    second_hop(0, 6)
+    second_hop(0, 7)
+    for q in range(PARTS[1]):
+        second_hop(1, q)
     carries = [
         lax.fori_loop(0, PARTS[g], functools.partial(finish, g), (jnp.zeros((count, 128), F32),) * 3)
         for g, (_, count) in enumerate(GROUPS)]
@@ -354,14 +372,11 @@
 
     with jax.named_scope("stats"):
         peak, violation, mass = carry
-        lane = lax.broadcasted_iota(jnp.int32, (share, 128), 1)
-        packed = jnp.where(
-            lane == 0, jnp.max(peak, axis=1, keepdims=True),
-            jnp.where(
-                lane == 1, jnp.sum(violation, axis=1, keepdims=True) * (1.0 / NF),
-                jnp.where(lane == 2, jnp.sum(mass, axis=1, keepdims=True) * (1.0 / NF), 0.0)))
-        packed = jnp.concatenate([packed, jnp.zeros((128 - share, 128), F32)], axis=0).T
-        peers[feat] = packed[:8, :]
+        column = jnp.concatenate([
+            jnp.max(peak, axis=1, keepdims=True), jnp.zeros((8, 1), F32),
+            jnp.sum(violation, axis=1, keepdims=True) * (1.0 / NF), jnp.zeros((8, 1), F32),
+            jnp.sum(mass, axis=1, keepdims=True) * (1.0 / NF), jnp.zeros((128 - 3 * share - 16, 1), F32)], axis=0)
+        peers[feat] = jnp.broadcast_to(column, (128, 128)).T[:1, :]
 
         def send_stats(k):
             return pltpu.make_async_remote_copy(
@@ -375,7 +390,7 @@
         for k in range(1, 16):
             largest = jnp.maximum(largest, everything[k])
             total = total + everything[k]
-        stats[...] = jnp.where(lax.broadcasted_iota(jnp.int32, (8, 128), 0) == 0, largest, total)
+        stats[...] = jnp.where(lax.broadcasted_iota(jnp.int32, (1, 128), 1) < share, largest, total)
 
     await_bytes(got1, sent.at[0])
     await_bytes(got1, sent.at[1])
@@ -399,7 +414,7 @@
         kernel,
         out_shape=(
             vmem((share, features), F32),
-            vmem((8, 128), F32),
+            vmem((1, 128), F32),
         ),
         in_specs=[everywhere] * 4 + [inside] * 2,
         out_specs=(inside, inside),
@@ -421,7 +436,7 @@
             vmem((2, share, features // 2), F32),
             vmem((2, share, features), F32),
             vmem((2, share, 128), F32),
-            vmem((16, 8, 128), F32),
+            vmem((16, 1, 128), F32),
             vmem((2 * height, 16 * GROUPS[0][1]), F32),
             dma((BLOCKS,)),
             dma((BLOCKS,)),
@@ -436,7 +451,7 @@
             collective_id=0, has_side_effects=True, vmem_limit_bytes=62 * 1024 * 1024
         ),
     )(design, coefficients, response, active_set, lambda_path.T, lambda_index.reshape(1, share))
-    return margins, stats[0, :share], stats[1, :share], stats[2, :share]
+    return margins, *(stats[0, k * (share + 8):k * (share + 8) + share] for k in range(3))
 
 
 def solution(mesh):

time: 54.6 us -> 53.2 us (0.974)
  Pallas kernels: 52.5 us -> 51.1 us
    pallas_call x1, Pallas kernels: 52.5 us -> 51.1 us  [body(): pl.pallas_call(kernel, out_shape=(vmem((share, features), F32), vmem((1,...]
where the time goes in v4:
time: 53.2 us; the launch traced here: 53.1 us
  Pallas kernels  51.1 us (96%)
  local copies, waits for them, and re-layouts  1.34 us (3%)
  between operations  0.64 us (1%)
    pallas_call x1, Pallas kernels, body(): pl.pallas_call(kernel, out_shape=(vmem((share, features), F32), vmem((1,...  51.1 us

profile of v4, /device:TPU:0, one launch (start us, length us, event | category | flops | bytes accessed | tf_op | source)
XLA Modules:
  0.0 53.1 jit_solution(11186972906097159878)
XLA Ops:
  0.6 51.1 %shard_map.93 = (f32[24,4096]{1,0:T(8,128)S(1)}, f32[1,128]{1,0:T(1,128)S(1)}) custom-call(f32[1024,4096]{1,0:T(8,128)} %design.1, f32[192,4096]{1,0:T(8,128)} %coefficients.1, f32[192,1024]{1,0:T(8,128)} %response.1, s32[192,4096]{1,0:T(8,128)} %active.1, f32[16,24]{1,0:T(8,128)} %bitcast.8, s32[1,24]{1,0:T(1,128)} %bitcast.9), custom_call_target="tpu_custom_call" | custom-call | tf_op jit(solution)/shard_map/pallas_call | solution.py:413
  51.7 0.7 %copy.11 = f32[24,4096]{1,0:T(8,128)} copy(f32[24,4096]{1,0:T(8,128)S(1)} %get-tuple-element.11) | data formatting | bytes 786432
  52.5 0.6 %slice_bitcast_fusion = (f32[24]{0:T(128)}, f32[24]{0:T(128)}, f32[24]{0:T(128)}) fusion(f32[1,128]{1,0:T(1,128)S(1)} %get-tuple-element.7), kind=kLoop, calls=%fused_computation | loop fusion | bytes 576 | tf_op jit(solution)/shard_map/squeeze | solution.py:454

commit v5 on v4

--- a/solution.py
+++ b/solution.py
@@ -30,7 +30,7 @@
     margins, stats,
     raw, d_all, coef, act, resp, m_a, m_b,
     part, got1, summed, got2, resid, a_a, a_b,
-    grad, got_core, got_hop, got_end, lams, peers, early,
+    grad, got_core, got_hop, got_end, lams, peers, early, path_v, index_v,
     coef_sem, act_sem, load_sem, sent, r1, r2, r3, rc, rx, rt,
 ):
     samp = lax.axis_index("samp")
@@ -80,6 +80,9 @@
             for load in load_block(b):
                 load.start()
 
+    load_small = (
+        pltpu.make_async_copy(lpath, path_v, load_sem.at[CHUNKS + 2]),
+        pltpu.make_async_copy(lindex, index_v, load_sem.at[CHUNKS + 3]))
     load_blocks(0)
     load_half(0).start()
 
@@ -88,18 +91,6 @@
         pl.semaphore_signal(barrier, inc=1, **to(samp, (feat + k) % 16))
     for s in (partner, left, right):
         pl.semaphore_signal(barrier, inc=1, **to(s, feat))
-
-    eye = lax.broadcasted_iota(jnp.int32, (share, share), 0) == lax.broadcasted_iota(jnp.int32, (share, share), 1)
-    positions = lax.broadcasted_iota(jnp.int32, lpath.shape, 0)
-    index, path = lindex[...], lpath[...]
-
-    def pick(chosen):
-        row = jnp.sum(jnp.where(positions == chosen, path, 0.0), axis=0, keepdims=True)
-        return jnp.sum(jnp.where(eye, jnp.broadcast_to(row, (share, share)), 0.0), axis=1, keepdims=True)
-
-    lam_new, lam_old = pick(index), pick(index - 1)
-    lams[0] = jnp.broadcast_to(lam_new, (share, 128))
-    lams[1] = jnp.broadcast_to(2.0 * lam_new - lam_old, (share, 128))
 
     @jax.named_scope("mask")
     def mask_step(b, carry):
@@ -219,6 +210,8 @@
     for c in range(3, CHUNKS):
         load_design(c).start()
     load_response.start()
+    for load in load_small:
+        load.start()
     pl.semaphore_wait(barrier, 18)
     start1(0, 0)
     lax.fori_loop(1, CHUNKS, fit_a, 0)
@@ -323,6 +316,20 @@
             phase2(1, CHUNKS - 1)
 
         return carry
+
+    for load in load_small:
+        load.wait()
+    eye = lax.broadcasted_iota(jnp.int32, (share, share), 0) == lax.broadcasted_iota(jnp.int32, (share, share), 1)
+    positions = lax.broadcasted_iota(jnp.int32, path_v.shape, 0)
+    index, path = index_v[...], path_v[...]
+
+    def pick(chosen):
+        row = jnp.sum(jnp.where(positions == chosen, path, 0.0), axis=0, keepdims=True)
+        return jnp.sum(jnp.where(eye, jnp.broadcast_to(row, (share, share)), 0.0), axis=1, keepdims=True)
+
+    lam_new, lam_old = pick(index), pick(index - 1)
+    lams[0] = jnp.broadcast_to(lam_new, (share, 128))
+    lams[1] = jnp.broadcast_to(2.0 * lam_new - lam_old, (share, 128))
 
     with jax.named_scope("phase12"):
         for c in range(CHUNKS):
@@ -416,7 +423,7 @@
             vmem((share, features), F32),
             vmem((1, 128), F32),
         ),
-        in_specs=[everywhere] * 4 + [inside] * 2,
+        in_specs=[everywhere] * 4 + [pl.BlockSpec(memory_space=pltpu.HBM)] * 2,
         out_specs=(inside, inside),
         scratch_shapes=[
             vmem((samples, features), F32),
@@ -438,9 +445,11 @@
             vmem((2, share, 128), F32),
             vmem((16, 1, 128), F32),
             vmem((2 * height, 16 * GROUPS[0][1]), F32),
+            vmem((lambda_path.shape[1], share), F32),
+            vmem((1, share), jnp.int32),
             dma((BLOCKS,)),
             dma((BLOCKS,)),
-            dma((CHUNKS + 2,)),
+            dma((CHUNKS + 4,)),
             dma((6,)),
             *[dma((2, CHUNKS))] * 3,
             dma((sum(PARTS),)),

time: 53.2 us -> 52.5 us (0.987)
  Pallas kernels: 51.1 us -> 50.4 us
    pallas_call x1, Pallas kernels: 51.1 us -> 50.4 us  [body(): pl.pallas_call(kernel, out_shape=(vmem((share, features), F32), vmem((1,...]
where the time goes in v5:
time: 52.5 us; the launch traced here: 52.4 us
  Pallas kernels  50.4 us (96%)
  local copies, waits for them, and re-layouts  1.34 us (3%)
  between operations  0.64 us (1%)
    pallas_call x1, Pallas kernels, body(): pl.pallas_call(kernel, out_shape=(vmem((share, features), F32), vmem((1,...  50.4 us

profile of v5, /device:TPU:0, one launch (start us, length us, event | category | flops | bytes accessed | tf_op | source)
XLA Modules:
  0.0 52.4 jit_solution(7413740420963705057)
XLA Ops:
  0.6 50.4 %shard_map.93 = (f32[24,4096]{1,0:T(8,128)S(1)}, f32[1,128]{1,0:T(1,128)S(1)}) custom-call(f32[1024,4096]{1,0:T(8,128)} %design.1, f32[192,4096]{1,0:T(8,128)} %coefficients.1, f32[192,1024]{1,0:T(8,128)} %response.1, s32[192,4096]{1,0:T(8,128)} %active.1, f32[16,24]{1,0:T(8,128)} %bitcast.8, s32[1,24]{1,0:T(1,128)} %bitcast.9), custom_call_target="tpu_custom_call" | custom-call | tf_op jit(solution)/shard_map/pallas_call | solution.py:420
  51.0 0.7 %copy.11 = f32[24,4096]{1,0:T(8,128)} copy(f32[24,4096]{1,0:T(8,128)S(1)} %get-tuple-element.11) | data formatting | bytes 786432
  51.8 0.6 %slice_bitcast_fusion = (f32[24]{0:T(128)}, f32[24]{0:T(128)}, f32[24]{0:T(128)}) fusion(f32[1,128]{1,0:T(1,128)S(1)} %get-tuple-element.7), kind=kLoop, calls=%fused_computation | loop fusion | bytes 576 | tf_op jit(solution)/shard_map/squeeze | solution.py:463
